TPU v7x, 32 devices: a whole 2x2x4 slice. The times are simulated.
32 devices in a mesh: dp: 8 (over z, y), tp: 4 (over x, core).
Axes of the slice: x: 2, y: 2, z: 4, core: 2. Of those that a mesh axis runs over, the one named last changes fastest.
Arguments:
- queries: bfloat16 [64, 16, 8192], P(('dp', 'tp')), parts along dimension 0, may hold values from -512 to 512
- kv_cache: bfloat16 [64, 8, 384, 256], P(('dp', 'tp')), parts along dimension 0, may hold values from -18 to 18
- lengths: int32 [64], P(('dp', 'tp')), parts along dimension 0, may hold values from 17 to 384, as said below
- residual: bfloat16 [64, 16, 8192], P(('dp', 'tp')), parts along dimension 0, may hold values from -4 to 4
- out_weight: bfloat16 [8192, 8192], P('tp'), may hold values from -0.0625 to 0.0625
- norm_gain: bfloat16 [8192], replicated, may hold values from 0.25 to 1.75
Outputs:
- hidden: bfloat16 [64, 16, 8192], P(('dp', 'tp')), parts along dimension 0
- normed: bfloat16 [64, 16, 8192], P(('dp', 'tp')), parts along dimension 0
There are 8 independent parts, one for each index of `dp`. A program takes and returns all parts, laid end to end along the dimension named above; an argument that names none is the same for every part. Nothing has to cross between parts.
Inputs may be any that keep to these rules, and one draw needn't show every extreme that they name: `lengths`: some sequence of every part has exactly 384 live slots.
All inputs are finite; a program needn't handle non-finite values.
Results may differ from a plain program's by a relative error of at most 0.015.
Values may be sent and summed in bfloat16 or wider, within the bound.
A program may use at most 128 MiB of HBM per device.

v0:
```python
import jax
import jax.numpy as jnp
from jax import lax
from jax.sharding import PartitionSpec as P

HEADS = 64
KV_HEADS = 8
HEAD_DIM = 128
DRAFT = 16
LEN = 384


def attend(queries, kv_cache, lengths):
    seq_count = queries.shape[0]
    per_group = HEADS // KV_HEADS
    grouped = queries.reshape(seq_count, DRAFT, KV_HEADS, per_group, HEAD_DIM).transpose(
        0, 2, 3, 1, 4
    )
    grouped = grouped.reshape(seq_count, KV_HEADS, per_group * DRAFT, HEAD_DIM)
    key_part = kv_cache[..., :HEAD_DIM]
    value_part = kv_cache[..., HEAD_DIM:]
    scores = jnp.einsum(
        "skqd,skld->skql", grouped, key_part, preferred_element_type=jnp.float32
    ) * HEAD_DIM ** (-0.5)
    draft_index = jnp.arange(per_group * DRAFT, dtype=jnp.int32) % DRAFT
    visible = lengths[:, None, None, None] - DRAFT + 1 + draft_index[None, None, :, None]
    position = jnp.arange(LEN, dtype=jnp.int32)
    allowed = position[None, None, None, :] < visible
    scores = jnp.where(allowed, scores, -1e30)
    peak = jnp.max(scores, axis=-1, keepdims=True)
    raised = jnp.exp(scores - peak)
    totals = jnp.sum(raised, axis=-1, keepdims=True)
    weights = (raised / totals).astype(jnp.bfloat16)
    attended = jnp.einsum(
        "skql,skld->skqd", weights, value_part, preferred_element_type=jnp.float32
    ).astype(jnp.bfloat16)
    attended = attended.reshape(seq_count, KV_HEADS, per_group, DRAFT, HEAD_DIM).transpose(
        0, 3, 1, 2, 4
    )
    return attended.reshape(seq_count, DRAFT, HEADS * HEAD_DIM)


def on_device(queries, kv_cache, lengths, residual, out_weight, norm_gain):
    attended = attend(queries, kv_cache, lengths)
    by_heads = lax.all_to_all(attended, "tp", split_axis=2, concat_axis=0, tiled=True)
    flat_rows = by_heads.reshape(-1, by_heads.shape[2])
    own_rows = lax.psum_scatter(
        jnp.dot(flat_rows, out_weight, preferred_element_type=jnp.float32).astype(jnp.bfloat16),
        "tp",
        scatter_dimension=0,
        tiled=True,
    ).astype(jnp.float32)
    summed = residual.astype(jnp.float32) + own_rows.reshape(residual.shape)
    hidden = summed.astype(jnp.bfloat16)
    scales = lax.rsqrt(jnp.mean(summed * summed, axis=-1, keepdims=True) + 1e-05)
    normed = (summed * scales * norm_gain.astype(jnp.float32)).astype(jnp.bfloat16)
    return (hidden, normed)


def solution(mesh):
    return jax.shard_map(
        on_device,
        mesh=mesh,
        in_specs=(
            P(("dp", "tp"), None, None),
            P(("dp", "tp"), None, None, None),
            P(("dp", "tp")),
            P(("dp", "tp"), None, None),
            P("tp", None),
            P(),
        ),
        out_specs=(P(("dp", "tp"), None, None), P(("dp", "tp"), None, None)),
        check_vma=False,
    )
```

profile of v0, /device:TPU:0, one launch (start us, length us, event | category | flops | bytes accessed | tf_op | source)
XLA Modules:
  0.0 112.8 jit_solution(9504903438683032021)
XLA Ops:
  7.2 0.0 reduce-scatter.2.cloned.1.call-start
  7.2 1.2 %copy.23 = bf16[4,8,64,128]{3,2,1,0:T(8,128)(2,1)S(1)} copy(bf16[4,8,64,128]{3,1,2,0:T(8,128)(2,1)} %bitcast.32) | data formatting | bytes 1048576
  8.4 0.3 copy.15
  8.7 0.7 broadcast_add_fusion.1
  9.4 0.1 broadcast_add_fusion
  9.5 0.1 iota_compare_fusion
  9.6 2.2 %fusion.6 = f32[2,8,128,384]{3,2,1,0:T(8,128)S(1)} fusion(bf16[2,8,128,128]{3,2,1,0:T(8,128)(2,1)S(1)} %bitcast.27, bf16[2,8,384,256]{3,2,1,0:T(8,128)(2,1)} %param.7), kind=kOutput, calls=%fused_computation.10 | convolution fusion | flops 201326592 | bytes 5242880 | tf_op jit(solution)/shard_map/skqd,skld->skql/dot_general | solution.py:22
  11.8 0.0 copy-start.1
  11.8 1.6 %fusion.15 = (f32[2,8,128]{2,1,0:T(8,128)S(1)}, f32[2,8,128,384]{3,2,1,0:T(8,128)S(1)}) fusion(f32[2,8,128,384]{3,2,1,0:T(8,128)S(1)} %fusion.6, pred[2,128,384]{2,1,0:T(8,128)(4,1)S(1)} %iota_compare_fusion), kind=kOutput, calls=%fused_computation.25 | output fusion | flops 4718975 | bytes 6397952 | tf_op jit(solution)/shard_map/sub | solution.py:31
  13.4 0.3 copy-done.1
  13.7 0.6 fusion.9
  14.3 7.2 %copy.20 = bf16[2,16,8,8,128]{1,0,4,3,2:T(2,128)(2,1)} copy(bf16[2,16,8,8,128]{4,1,3,2,0:T(8,128)(2,1)S(1)} %bitcast.31) | data formatting | bytes 1048576 | tf_op jit(solution)/shard_map/reshape | solution.py:40
  21.6 5.8 %reshape.96 = bf16[4,2,32768]{2,1,0:T(2,128)(2,1)S(1)} reshape(bf16[8192,2,16]{2,1,0:T(2,128)(2,1)} %bitcast.24) | data formatting | bytes 1048576
  27.3 12.9 %all_to_all.15 = bf16[4,2,32768]{2,1,0:T(2,128)(2,1)S(1)} all-to-all(bf16[4,2,32768]{2,1,0:T(2,128)(2,1)S(1)} %reshape.96), channel_id=1, replica_groups=mesh['dp'=8,'tp'=4] {'tp'}, dimensions={0} | all-to-all | bytes 1048576 | tf_op jit(solution)/shard_map/all_to_all | solution.py:45
  40.2 4.1 %reshape.97 = bf16[8192,2,16]{2,1,0:T(2,128)(2,1)} reshape(bf16[4,2,32768]{2,1,0:T(2,128)(2,1)S(1)} %all_to_all.15) | data formatting | bytes 1048576
  44.3 9.7 %copy.21 = bf16[2,16,4,2048]{3,2,1,0:T(4,128)(2,1)S(1)} copy(bf16[2,16,4,2048]{1,0,3,2:T(2,128)(2,1)} %bitcast.25) | data formatting | bytes 1048576 | tf_op jit(solution)/shard_map/all_to_all | solution.py:45
  54.0 0.3 copy.19
  54.3 0.0 copy-start.2
  54.3 0.0 copy-start
  54.3 16.5 %convolution_convert_fusion = bf16[128,8192]{1,0:T(8,128)(2,1)} fusion(bf16[128,2048]{1,0:T(8,128)(2,1)S(1)} %bitcast.26, bf16[2048,8192]{1,0:T(8,128)(2,1)} %param.10), kind=kOutput, calls=%fused_computation.1 | convolution fusion | flops 4296015872 | bytes 36175872 | tf_op jit(solution)/shard_map/dot_general | solution.py:48
  70.8 0.0 reduce-scatter.2.cloned.1.call-update
  70.9 31.6 %reduce-scatter.2.cloned.1.call-done = bf16[32,8192]{1,0:T(8,128)(2,1)} async-done(((bf16[128,8192]{1,0:T(8,128)(2,1)}), bf16[32,8192]{1,0:T(8,128)(2,1)}) %reduce-scatter.2.cloned.1.call-update) | async-done | bytes 524304 | tf_op jit(solution)/shard_map/reduce_scatter | solution.py:47
  102.5 1.3 %multiply_reduce_fusion = f32[2,16]{1,0:T(2,128)S(1)} fusion(bf16[2,16,8192]{2,1,0:T(8,128)(2,1)} %bitcast.29, bf16[2,16,8192]{2,1,0:T(8,128)(2,1)S(1)} %copy-done), kind=kLoop, calls=%fused_computation.16 | loop fusion | flops 1310688 | bytes 1048704 | tf_op jit(solution)/shard_map/reduce_sum | solution.py:55
  103.8 2.2 %multiply_convert_fusion = (bf16[2,16,8192]{2,1,0:T(8,128)(2,1)}, bf16[2,16,8192]{2,1,0:T(8,128)(2,1)}) fusion(bf16[2,16,8192]{2,1,0:T(8,128)(2,1)S(1)} %copy-done, f32[8192]{0:T(1024)S(1)} %convert_element_type.27, f32[2,16]{1,0:T(2,128)S(1)} %add_rsqrt_fusion, bf16[32,8192]{1,0:T(8,128)(2,1)} %reduce-scatter.2.cloned.1.call-done), kind=kLoop, calls=%fused_computation.15 | loop fusion | flops 1835008 | bytes 2130048 | tf_op jit(solution)/shard_map/convert_element_type | solution.py:56
  (5 shorter events, 0.0 us)
Async XLA Ops:
  7.2 95.3 %reduce-scatter.2.cloned.1.call-start = ((), (), s32[]{:S(2)}) async-start(), calls=%async_computation.2 | async-start | bytes 2621440 | tf_op jit(solution)/shard_map/reduce_scatter | solution.py:47
  11.8 1.9 %copy-start.1 = (bf16[2,8,384,256]{3,2,1,0:T(8,128)(2,1)S(1)}, bf16[2,8,384,256]{3,2,1,0:T(8,128)(2,1)}, u32[]{:S(2)}) copy-start(bf16[2,8,384,256]{3,2,1,0:T(8,128)(2,1)} %param.7) | copy-start | bytes 9437188
  54.3 16.6 %copy-start.2 = (bf16[8192]{0:T(1024)(128)(2,1)S(1)}, bf16[8192]{0:T(1024)(128)(2,1)}, u32[]{:S(2)}) copy-start(bf16[8192]{0:T(1024)(128)(2,1)} %param.11) | copy-start | bytes 49156
  54.3 48.2 %copy-start = (bf16[2,16,8192]{2,1,0:T(8,128)(2,1)S(1)}, bf16[2,16,8192]{2,1,0:T(8,128)(2,1)}, u32[]{:S(2)}) copy-start(bf16[2,16,8192]{2,1,0:T(8,128)(2,1)} %param.9) | copy-start | bytes 1572868
Sparse Core Ops, SparseCore 0:
  71.0 31.4 reduce-scatter.1
where the time goes:
time: 113 us
  waiting for transfers between devices  31.6 us (28%)
  local copies, waits for them, and re-layouts  28.9 us (26%)
  matrix products  19.3 us (17%)
  between operations  14.1 us (12%)
  blocking collectives  12.9 us (11%)
  other arithmetic  5.96 us (5%)
    reduce_scatter x1, waiting for transfers between devices, on_device(): lax.psum_scatter(jnp.dot(flat_rows, out_weight, preferred_element_type=jn...  31.6 us
    dot_general x1, matrix products, on_device(): jnp.dot(flat_rows, out_weight, preferred_element_type=jnp.float32)  16.5 us
    all_to_all x1, blocking collectives, on_device(): lax.all_to_all(attended, 'tp', split_axis=2, concat_axis=0, tiled=True)  12.9 us
    unnamed x9, local copies, waits for them, and re-layouts  11.4 us
    all_to_all x2, local copies, waits for them, and re-layouts, on_device(): lax.all_to_all(attended, 'tp', split_axis=2, concat_axis=0, tiled=True)  9.96 us
    reshape x1, local copies, waits for them, and re-layouts, attend(): return attended.reshape(seq_count, DRAFT, HEADS * HEAD_DIM)  7.25 us
  transfers between devices with their start and end apart: 1, of which 1 were waited for; matrix products, arithmetic and copies ran while one was open for 0% of the time, Pallas kernels for 0%

commit v1 on v0

v1 whole, which is shorter than its diff:
```python
import functools
import math

import jax
import jax.numpy as jnp
from jax import lax
from jax.experimental import pallas as pl
from jax.experimental.pallas import tpu as pltpu
from jax.sharding import PartitionSpec as P

CORES = 2
COLUMNS = 512
LANES = 128


def block_kernel(
    n,
    lengths_ref,
    queries_ref,
    kv_ref,
    residual_ref,
    weight_ref,
    gain_ref,
    hidden_ref,
    normed_ref,
    q_buf,
    kv_buf,
    res_buf,
    w_buf,
    gain_buf,
    att_send,
    att,
    keep,
    mate_send,
    mate_recv,
    cross_send,
    cross_recv,
    acc,
    hidden_buf,
    normed_buf,
    load_sem,
    kv_sem,
    w_sem,
    att_send_sem,
    att_recv_sem,
    mate_send_sem,
    mate_recv_sem,
    cross_send_sem,
    cross_recv_sem,
    out_sem,
):
    chips = n // CORES
    seqs, draft, width = queries_ref.shape
    kv_heads, slots_kv, head_dim = kv_ref.shape[1], kv_ref.shape[2], kv_ref.shape[3] // 2
    heads = width // head_dim
    group = heads // kv_heads
    own_heads = heads // n
    unit_heads = min(own_heads, group)
    units = own_heads // unit_heads
    kv_per_dest = kv_buf.shape[2]
    rows = seqs * draft
    chunks, depth, columns = w_buf.shape
    model = chunks * columns

    me = lax.axis_index("tp")
    chip, core = me // CORES, me % CORES

    def device(dx, dk):
        return ((chip + dx) % chips) * CORES + (core + dk) % CORES

    def slot_of(dx, dk):
        return dx * CORES + dk

    order = [(dx, dk) for dx in range(1, chips) for dk in range(CORES)] + [(0, 1), (0, 0)]

    q_copy = pltpu.make_async_copy(queries_ref, q_buf, load_sem.at[0])
    q_copy.start()
    kv_copies = []
    for step, (dx, dk) in enumerate(order):
        first = device(dx, dk) * own_heads // group
        copy = pltpu.make_async_copy(
            kv_ref.at[:, pl.ds(first, kv_per_dest)], kv_buf.at[step], kv_sem.at[step]
        )
        copy.start()
        kv_copies.append(copy)

    def w_copy(c):
        at = pl.multiple_of(c * columns, LANES)
        return pltpu.make_async_copy(
            weight_ref.at[:, pl.ds(at, columns)], w_buf.at[c], w_sem.at[c]
        )

    def start_w(c, carry):
        w_copy(c).start()
        return carry

    lax.fori_loop(0, chunks, start_w, 0)
    res_copy = pltpu.make_async_copy(residual_ref, res_buf, load_sem.at[1])
    res_copy.start()
    gain_copy = pltpu.make_async_copy(gain_ref, gain_buf, load_sem.at[2])
    gain_copy.start()

    barrier = pltpu.get_barrier_semaphore()
    for dx, dk in order[:-1]:
        pl.semaphore_signal(
            barrier,
            inc=1,
            device_id={"tp": device(dx, dk)},
            device_id_type=pl.DeviceIdType.MESH,
        )
    pl.semaphore_wait(barrier, n - 1)

    q_copy.wait()
    position = lax.broadcasted_iota(jnp.int32, (draft, slots_kv), 1)
    token = lax.broadcasted_iota(jnp.int32, (draft, slots_kv), 0)
    biases = [
        jnp.where(position < lengths_ref[s] - draft + 1 + token, 0.0, -1e30).astype(jnp.float32)
        for s in range(seqs)
    ]
    factor = head_dim ** (-0.5) * math.log2(math.e)

    def att_copy(dx, dk, s, source_slot, target_slot):
        part = pl.ds(s * draft, draft)
        return pltpu.make_async_remote_copy(
            src_ref=att_send.at[source_slot, part],
            dst_ref=att.at[target_slot, part],
            send_sem=att_send_sem.at[source_slot, s],
            recv_sem=att_recv_sem.at[target_slot, s],
            device_id={"tp": device(dx, dk)},
            device_id_type=pl.DeviceIdType.MESH,
        )

    for step, (dx, dk) in enumerate(order):
        slot = slot_of(dx, dk)
        dest = device(dx, dk)
        kv_copies[step].wait()
        target = att if slot == 0 else att_send
        for s in range(seqs):
            for u in range(units):
                kv_at = u if own_heads >= group else 0
                start = pl.multiple_of((dest * own_heads + u * unit_heads) * head_dim, LANES)
                wide = q_buf[s, :, pl.ds(start, unit_heads * head_dim)]
                q_rows = jnp.concatenate(
                    [wide[:, h * head_dim : (h + 1) * head_dim] for h in range(unit_heads)], axis=0
                )
                keys = kv_buf[step, s, kv_at, :, :head_dim]
                values = kv_buf[step, s, kv_at, :, head_dim:]
                scores = lax.dot_general(
                    q_rows, keys, (((1,), (1,)), ((), ())), preferred_element_type=jnp.float32
                )
                scores = scores.reshape(unit_heads, draft, slots_kv) + biases[s][None]
                peak = jnp.max(scores, axis=-1, keepdims=True)
                raised = jnp.exp2((scores - peak) * factor)
                totals = jnp.sum(raised, axis=-1, keepdims=True)
                out = jnp.dot(
                    raised.astype(jnp.bfloat16).reshape(unit_heads * draft, slots_kv),
                    values,
                    preferred_element_type=jnp.float32,
                )
                out = (out * (1.0 / totals).reshape(unit_heads * draft, 1)).astype(jnp.bfloat16)
                for h in range(unit_heads):
                    at = (u * unit_heads + h) * head_dim
                    target[slot, s * draft : (s + 1) * draft, at : at + head_dim] = out[
                        h * draft : (h + 1) * draft
                    ]
            if slot:
                att_copy(dx, dk, s, slot, slot_of((chips - dx) % chips, dk)).start()

    for dx, dk in order[:-1]:
        slot = slot_of(dx, dk)
        for s in range(seqs):
            att_copy(dx, dk, s, slot, slot).wait_recv()

    def mate_copy(c):
        return pltpu.make_async_remote_copy(
            src_ref=mate_send.at[c],
            dst_ref=mate_recv.at[c],
            send_sem=mate_send_sem.at[c],
            recv_sem=mate_recv_sem.at[c],
            device_id={"tp": device(0, 1)},
            device_id_type=pl.DeviceIdType.MESH,
        )

    def cross_copy(dx, source, target, c):
        return pltpu.make_async_remote_copy(
            src_ref=cross_send.at[source, c],
            dst_ref=cross_recv.at[target, c],
            send_sem=cross_send_sem.at[source, c],
            recv_sem=cross_recv_sem.at[target, c],
            device_id={"tp": device(dx, 0)},
            device_id_type=pl.DeviceIdType.MESH,
        )

    def multiply(c):
        w_copy(c).wait()
        product = jnp.dot(
            att[...].reshape(n * rows, depth), w_buf[c], preferred_element_type=jnp.float32
        )
        for dx in range(chips):
            own, other = slot_of(dx, 0) * rows, slot_of(dx, 1) * rows
            mate_send[c, dx] = product[other : other + rows].astype(jnp.bfloat16)
            keep[c % 2, dx] = product[own : own + rows]
        mate_copy(c).start()

    def pass_on(c):
        mate_copy(c).wait_recv()
        for dx in range(1, chips):
            both = keep[c % 2, dx] + mate_recv[c, dx].astype(jnp.float32)
            cross_send[dx - 1, c] = both.astype(jnp.bfloat16)
            cross_copy(dx, dx - 1, chips - dx - 1, c).start()
        acc[c] = keep[c % 2, 0] + mate_recv[c, 0].astype(jnp.float32)

    multiply(0)

    def both_steps(c, carry):
        multiply(c)
        pass_on(c - 1)
        return carry

    lax.fori_loop(1, chunks, both_steps, 0)
    pass_on(chunks - 1)

    res_copy.wait()

    def collect(c, squares):
        at = pl.multiple_of(c * columns, LANES)
        total = acc[c]
        for dx in range(1, chips):
            cross_copy(dx, dx - 1, dx - 1, c).wait_recv()
            total = total + cross_recv[dx - 1, c].astype(jnp.float32)
        total = total + res_buf[:, :, pl.ds(at, columns)].astype(jnp.float32).reshape(rows, columns)
        acc[c] = total
        hidden_buf[:, :, pl.ds(at, columns)] = total.astype(jnp.bfloat16).reshape(
            seqs, draft, columns
        )
        for tile in range(columns // LANES):
            part = total[:, tile * LANES : (tile + 1) * LANES]
            squares = squares + part * part
        return squares

    squares = lax.fori_loop(0, chunks, collect, jnp.zeros((rows, LANES), jnp.float32))
    hidden_copy = pltpu.make_async_copy(hidden_buf, hidden_ref, out_sem.at[0])
    hidden_copy.start()
    scales = lax.rsqrt(jnp.sum(squares, axis=-1, keepdims=True) / model + 1e-05)
    gain_copy.wait()

    def normalize(c, carry):
        at = pl.multiple_of(c * columns, LANES)
        gain = gain_buf[:, pl.ds(at, columns)].astype(jnp.float32)
        normed = (acc[c] * scales * gain).astype(jnp.bfloat16)
        normed_buf[:, :, pl.ds(at, columns)] = normed.reshape(seqs, draft, columns)
        return carry

    lax.fori_loop(0, chunks, normalize, 0)
    normed_copy = pltpu.make_async_copy(normed_buf, normed_ref, out_sem.at[1])
    normed_copy.start()

    for dx, dk in order[:-1]:
        slot = slot_of(dx, dk)
        for s in range(seqs):
            att_copy(dx, dk, s, slot, slot).wait_send()

    def settle(c, carry):
        mate_copy(c).wait_send()
        for dx in range(1, chips):
            cross_copy(dx, dx - 1, dx - 1, c).wait_send()
        return carry

    lax.fori_loop(0, chunks, settle, 0)
    hidden_copy.wait()
    normed_copy.wait()


def on_device(n, queries, kv_cache, lengths, residual, out_weight, norm_gain):
    seqs, draft, width = queries.shape
    kv_heads, slots_kv, pair_dim = kv_cache.shape[1:]
    head_dim = pair_dim // 2
    heads = width // head_dim
    depth, model = out_weight.shape
    chips = n // CORES
    rows = seqs * draft
    columns = math.gcd(model, COLUMNS)
    chunks = model // columns
    kv_per_dest = max(1, kv_heads // n)
    bf16, f32 = jnp.bfloat16, jnp.float32
    dma = pltpu.SemaphoreType.DMA
    out = jax.ShapeDtypeStruct(residual.shape, bf16)
    return pl.pallas_call(
        functools.partial(block_kernel, n),
        out_shape=(out, out),
        in_specs=[pl.BlockSpec(memory_space=pltpu.SMEM)]
        + [pl.BlockSpec(memory_space=pl.ANY)] * 5,
        out_specs=[pl.BlockSpec(memory_space=pl.ANY)] * 2,
        scratch_shapes=[
            pltpu.VMEM(queries.shape, bf16),
            pltpu.VMEM((n, seqs, kv_per_dest, slots_kv, pair_dim), bf16),
            pltpu.VMEM(residual.shape, bf16),
            pltpu.VMEM((chunks, depth, columns), bf16),
            pltpu.VMEM((1, model), bf16),
            pltpu.VMEM((n, rows, depth), bf16),
            pltpu.VMEM((n, rows, depth), bf16),
            pltpu.VMEM((2, chips, rows, columns), f32),
            pltpu.VMEM((chunks, chips, rows, columns), bf16),
            pltpu.VMEM((chunks, chips, rows, columns), bf16),
            pltpu.VMEM((max(1, chips - 1), chunks, rows, columns), bf16),
            pltpu.VMEM((max(1, chips - 1), chunks, rows, columns), bf16),
            pltpu.VMEM((chunks, rows, columns), f32),
            pltpu.VMEM(residual.shape, bf16),
            pltpu.VMEM(residual.shape, bf16),
            dma((3,)),
            dma((n,)),
            dma((chunks,)),
            dma((n, seqs)),
            dma((n, seqs)),
            dma((chunks,)),
            dma((chunks,)),
            dma((max(1, chips - 1), chunks)),
            dma((max(1, chips - 1), chunks)),
            dma((2,)),
        ],
        compiler_params=pltpu.CompilerParams(
            collective_id=0, has_side_effects=True, vmem_limit_bytes=60 * 1024 * 1024
        ),
    )(lengths, queries, kv_cache, residual, out_weight, norm_gain.reshape(1, model))


def solution(mesh):
    return jax.shard_map(
        functools.partial(on_device, mesh.shape["tp"]),
        mesh=mesh,
        in_specs=(
            P(("dp", "tp"), None, None),
            P(("dp", "tp"), None, None, None),
            P(("dp", "tp")),
            P(("dp", "tp"), None, None),
            P("tp", None),
            P(),
        ),
        out_specs=(P(("dp", "tp"), None, None), P(("dp", "tp"), None, None)),
        check_vma=False,
    )
```

time: 113 us -> 35 us (0.31)
  waiting for transfers between devices: 31.6 us -> 0 us
  Pallas kernels: 0 us -> 29 us
  local copies, waits for them, and re-layouts: 28.9 us -> 5.09 us
  matrix products: 19.3 us -> 0 us
  between operations: 14.1 us -> 0.64 us
  blocking collectives: 12.9 us -> 0 us
  other arithmetic: 5.96 us -> 0 us
    reduce_scatter x1 -> x0, waiting for transfers between devices: 31.6 us -> none  [on_device(): lax.psum_scatter(jnp.dot(flat_rows, out_weight, preferred_element_type=jn...]
    pallas_call x0 -> x1, Pallas kernels: none -> 29 us  [on_device(): pl.pallas_call(functools.partial(block_kernel, n), out_shape=(out, out),...]
    dot_general x3 -> x0, matrix products: 19.3 us -> none  [the longest x1 16.5 us: on_device(): jnp.dot(flat_rows, out_weight, preferred_element_type=jnp.float32)]
    all_to_all x1 -> x0, blocking collectives: 12.9 us -> none  [on_device(): lax.all_to_all(attended, 'tp', split_axis=2, concat_axis=0, tiled=True)]
    all_to_all x2 -> x0, local copies, waits for them, and re-layouts: 9.96 us -> none  [on_device(): lax.all_to_all(attended, 'tp', split_axis=2, concat_axis=0, tiled=True)]
    unnamed x9 -> x2, local copies, waits for them, and re-layouts: 11.4 us -> 3.74 us
    reshape x1, local copies, waits for them, and re-layouts: 7.25 us -> 1.35 us  [on_device(): norm_gain.reshape(1, model)]
    convert_element_type x2 -> x0, other arithmetic: 2.23 us -> none  [the longest x1 2.22 us: on_device(): (summed * scales * norm_gain.astype(jnp.float32)).astype(jnp.bfloat16)]
  transfers between devices with their start and end apart: 1 -> 0, of which waited for: 1 -> 0; matrix products, arithmetic and copies ran while one was open for 0% -> 0% of each run, Pallas kernels for 0% -> 0%
where the time goes in v1:
time: 35 us; the launch traced here: 34.7 us
  Pallas kernels  29 us (83%)
  local copies, waits for them, and re-layouts  5.09 us (15%)
  between operations  0.64 us (2%)
    pallas_call x1, Pallas kernels, on_device(): pl.pallas_call(functools.partial(block_kernel, n), out_shape=(out, out),...  29 us
    unnamed x2, local copies, waits for them, and re-layouts  3.74 us
    reshape x1, local copies, waits for them, and re-layouts, on_device(): norm_gain.reshape(1, model)  1.35 us

profile of v1, /device:TPU:0, one launch (start us, length us, event | category | flops | bytes accessed | tf_op | source)
XLA Modules:
  0.0 34.7 jit_solution(2747504391383551001)
XLA Ops:
  0.6 1.4 %reshape.7.gain_ref = bf16[1,8192]{1,0:T(2,128)(2,1)} reshape(bf16[8192]{0:T(1024)(128)(2,1)} %param.11) | data formatting | bytes 32768 | tf_op jit(solution)/shard_map/reshape | solution.py:324
  2.0 29.0 %shard_map.77 = (bf16[2,16,8192]{2,1,0:T(8,128)(2,1)}, bf16[2,16,8192]{2,1,0:T(8,128)(2,1)}) custom-call(s32[2]{0:T(128)} %lengths_ref.1, bf16[2,16,8192]{2,1,0:T(8,128)(2,1)} %queries_ref.1, bf16[2,8,384,256]{3,2,1,0:T(8,128)(2,1)} %kv_ref.1, bf16[2,16,8192]{2,1,0:T(8,128)(2,1)} %residual_ref.1, bf16[2048,8192]{1,0:T(8,128)(2,1)} %weight_ref.1, ...), custom_call_target="tpu_custom_call" | custom-call | tf_op jit(solution)/shard_map/pallas_call | solution.py:288
  30.9 1.9 %copy.10 = bf16[2,16,8192]{2,1,0:T(8,128)(2,1)} copy(bf16[2,16,8192]{2,1,0:T(8,128)(2,1)} %get-tuple-element.4) | data formatting | bytes 1048576
  32.8 1.9 %copy.11 = bf16[2,16,8192]{2,1,0:T(8,128)(2,1)} copy(bf16[2,16,8192]{2,1,0:T(8,128)(2,1)} %get-tuple-element.5) | data formatting | bytes 1048576

commit v2 on v1

--- a/solution.py
+++ b/solution.py
@@ -20,14 +20,12 @@
     kv_ref,
     residual_ref,
     weight_ref,
-    gain_ref,
-    hidden_ref,
-    normed_ref,
+    acc,
+    scaled_ref,
     q_buf,
     kv_buf,
     res_buf,
     w_buf,
-    gain_buf,
     att_send,
     att,
     keep,
@@ -35,9 +33,6 @@
     mate_recv,
     cross_send,
     cross_recv,
-    acc,
-    hidden_buf,
-    normed_buf,
     load_sem,
     kv_sem,
     w_sem,
@@ -47,7 +42,6 @@
     mate_recv_sem,
     cross_send_sem,
     cross_recv_sem,
-    out_sem,
 ):
     chips = n // CORES
     seqs, draft, width = queries_ref.shape
@@ -97,8 +91,6 @@
     lax.fori_loop(0, chunks, start_w, 0)
     res_copy = pltpu.make_async_copy(residual_ref, res_buf, load_sem.at[1])
     res_copy.start()
-    gain_copy = pltpu.make_async_copy(gain_ref, gain_buf, load_sem.at[2])
-    gain_copy.start()
 
     barrier = pltpu.get_barrier_semaphore()
     for dx, dk in order[:-1]:
@@ -208,7 +200,9 @@
             both = keep[c % 2, dx] + mate_recv[c, dx].astype(jnp.float32)
             cross_send[dx - 1, c] = both.astype(jnp.bfloat16)
             cross_copy(dx, dx - 1, chips - dx - 1, c).start()
-        acc[c] = keep[c % 2, 0] + mate_recv[c, 0].astype(jnp.float32)
+        at = pl.multiple_of(c * columns, LANES)
+        own = keep[c % 2, 0] + mate_recv[c, 0].astype(jnp.float32)
+        acc[:, :, pl.ds(at, columns)] = own.reshape(seqs, draft, columns)
 
     multiply(0)
 
@@ -224,36 +218,27 @@
 
     def collect(c, squares):
         at = pl.multiple_of(c * columns, LANES)
-        total = acc[c]
+        total = acc[:, :, pl.ds(at, columns)]
         for dx in range(1, chips):
             cross_copy(dx, dx - 1, dx - 1, c).wait_recv()
-            total = total + cross_recv[dx - 1, c].astype(jnp.float32)
-        total = total + res_buf[:, :, pl.ds(at, columns)].astype(jnp.float32).reshape(rows, columns)
-        acc[c] = total
-        hidden_buf[:, :, pl.ds(at, columns)] = total.astype(jnp.bfloat16).reshape(
-            seqs, draft, columns
-        )
+            part = cross_recv[dx - 1, c].astype(jnp.float32)
+            total = total + part.reshape(seqs, draft, columns)
+        total = total + res_buf[:, :, pl.ds(at, columns)].astype(jnp.float32)
+        acc[:, :, pl.ds(at, columns)] = total
         for tile in range(columns // LANES):
-            part = total[:, tile * LANES : (tile + 1) * LANES]
+            part = total[:, :, tile * LANES : (tile + 1) * LANES]
             squares = squares + part * part
         return squares
 
-    squares = lax.fori_loop(0, chunks, collect, jnp.zeros((rows, LANES), jnp.float32))
-    hidden_copy = pltpu.make_async_copy(hidden_buf, hidden_ref, out_sem.at[0])
-    hidden_copy.start()
+    squares = lax.fori_loop(0, chunks, collect, jnp.zeros((seqs, draft, LANES), jnp.float32))
     scales = lax.rsqrt(jnp.sum(squares, axis=-1, keepdims=True) / model + 1e-05)
-    gain_copy.wait()
-
-    def normalize(c, carry):
+
+    def scale(c, carry):
         at = pl.multiple_of(c * columns, LANES)
-        gain = gain_buf[:, pl.ds(at, columns)].astype(jnp.float32)
-        normed = (acc[c] * scales * gain).astype(jnp.bfloat16)
-        normed_buf[:, :, pl.ds(at, columns)] = normed.reshape(seqs, draft, columns)
+        scaled_ref[:, :, pl.ds(at, columns)] = acc[:, :, pl.ds(at, columns)] * scales
         return carry
 
-    lax.fori_loop(0, chunks, normalize, 0)
-    normed_copy = pltpu.make_async_copy(normed_buf, normed_ref, out_sem.at[1])
-    normed_copy.start()
+    lax.fori_loop(0, chunks, scale, 0)
 
     for dx, dk in order[:-1]:
         slot = slot_of(dx, dk)
@@ -267,8 +252,6 @@
         return carry
 
     lax.fori_loop(0, chunks, settle, 0)
-    hidden_copy.wait()
-    normed_copy.wait()
 
 
 def on_device(n, queries, kv_cache, lengths, residual, out_weight, norm_gain):
@@ -284,19 +267,20 @@
     kv_per_dest = max(1, kv_heads // n)
     bf16, f32 = jnp.bfloat16, jnp.float32
     dma = pltpu.SemaphoreType.DMA
-    out = jax.ShapeDtypeStruct(residual.shape, bf16)
-    return pl.pallas_call(
+    summed, scaled = pl.pallas_call(
         functools.partial(block_kernel, n),
-        out_shape=(out, out),
+        out_shape=(
+            pltpu.VMEM(residual.shape, f32),
+            pltpu.VMEM(residual.shape, f32),
+        ),
         in_specs=[pl.BlockSpec(memory_space=pltpu.SMEM)]
-        + [pl.BlockSpec(memory_space=pl.ANY)] * 5,
-        out_specs=[pl.BlockSpec(memory_space=pl.ANY)] * 2,
+        + [pl.BlockSpec(memory_space=pl.ANY)] * 4,
+        out_specs=[pl.BlockSpec(memory_space=pltpu.VMEM)] * 2,
         scratch_shapes=[
             pltpu.VMEM(queries.shape, bf16),
             pltpu.VMEM((n, seqs, kv_per_dest, slots_kv, pair_dim), bf16),
             pltpu.VMEM(residual.shape, bf16),
             pltpu.VMEM((chunks, depth, columns), bf16),
-            pltpu.VMEM((1, model), bf16),
             pltpu.VMEM((n, rows, depth), bf16),
             pltpu.VMEM((n, rows, depth), bf16),
             pltpu.VMEM((2, chips, rows, columns), f32),
@@ -304,10 +288,7 @@
             pltpu.VMEM((chunks, chips, rows, columns), bf16),
             pltpu.VMEM((max(1, chips - 1), chunks, rows, columns), bf16),
             pltpu.VMEM((max(1, chips - 1), chunks, rows, columns), bf16),
-            pltpu.VMEM((chunks, rows, columns), f32),
-            pltpu.VMEM(residual.shape, bf16),
-            pltpu.VMEM(residual.shape, bf16),
-            dma((3,)),
+            dma((2,)),
             dma((n,)),
             dma((chunks,)),
             dma((n, seqs)),
@@ -316,12 +297,13 @@
             dma((chunks,)),
             dma((max(1, chips - 1), chunks)),
             dma((max(1, chips - 1), chunks)),
-            dma((2,)),
         ],
         compiler_params=pltpu.CompilerParams(
-            collective_id=0, has_side_effects=True, vmem_limit_bytes=60 * 1024 * 1024
+            collective_id=0, has_side_effects=True, vmem_limit_bytes=56 * 1024 * 1024
         ),
-    )(lengths, queries, kv_cache, residual, out_weight, norm_gain.reshape(1, model))
+    )(lengths, queries, kv_cache, residual, out_weight)
+    normed = scaled * norm_gain.astype(f32)
+    return summed.astype(bf16), normed.astype(bf16)
 
 
 def solution(mesh):

time: 35 us -> 30.8 us (0.88)
  local copies, waits for them, and re-layouts: 5.09 us -> 0.01 us
  other arithmetic: 0 us -> 1.71 us
  Pallas kernels: 29 us -> 28.3 us
    unnamed x2, local copies, waits for them, and re-layouts: 3.74 us -> 0.01 us
    convert_element_type x0 -> x3, other arithmetic: none -> 1.71 us  [the longest x2 1.71 us: on_device(): return (summed.astype(bf16), normed.astype(bf16))]
    reshape x1 -> x0, local copies, waits for them, and re-layouts: 1.35 us -> none  [on_device(): norm_gain.reshape(1, model)]
    pallas_call x1, Pallas kernels: 29 us -> 28.3 us  [on_device(): pl.pallas_call(functools.partial(block_kernel, n), out_shape=(pltpu.VMEM(...]
where the time goes in v2:
time: 30.8 us; the launch traced here: 30.7 us
  Pallas kernels  28.3 us (92%)
  other arithmetic  1.71 us (6%)
  between operations  0.65 us (2%)
    pallas_call x1, Pallas kernels, on_device(): pl.pallas_call(functools.partial(block_kernel, n), out_shape=(pltpu.VMEM(...  28.3 us
    convert_element_type x2, other arithmetic, on_device(): return (summed.astype(bf16), normed.astype(bf16))  1.71 us

profile of v2, /device:TPU:0, one launch (start us, length us, event | category | flops | bytes accessed | tf_op | source)
XLA Modules:
  0.0 30.7 jit_solution(16768082838318897704)
XLA Ops:
  0.6 0.0 copy-start
  0.6 28.3 %shard_map.77 = (f32[2,16,8192]{2,1,0:T(8,128)S(1)}, f32[2,16,8192]{2,1,0:T(8,128)S(1)}) custom-call(s32[2]{0:T(128)} %lengths_ref.1, bf16[2,16,8192]{2,1,0:T(8,128)(2,1)} %queries_ref.1, bf16[2,8,384,256]{3,2,1,0:T(8,128)(2,1)} %kv_ref.1, bf16[2,16,8192]{2,1,0:T(8,128)(2,1)} %residual_ref.1, bf16[2048,8192]{1,0:T(8,128)(2,1)} %weight_ref.1), custom_call_target="tpu_custom_call" | custom-call | tf_op jit(solution)/shard_map/pallas_call | solution.py:270
  28.9 0.8 %convert_element_type.9 = bf16[2,16,8192]{2,1,0:T(8,128)(2,1)} convert(f32[2,16,8192]{2,1,0:T(8,128)S(1)} %get-tuple-element.4) | non-fusion elementwise | flops 262144 | bytes 1572864 | tf_op jit(solution)/shard_map/convert_element_type | solution.py:306
  29.8 0.0 copy-done
  29.8 0.9 %multiply_convert_fusion = bf16[2,16,8192]{2,1,0:T(8,128)(2,1)} fusion(f32[2,16,8192]{2,1,0:T(8,128)S(1)} %get-tuple-element.5, f32[8192]{0:T(1024)S(1)} %convert_element_type.10), kind=kLoop, calls=%fused_computation | loop fusion | flops 524288 | bytes 1605632 | tf_op jit(solution)/shard_map/convert_element_type | solution.py:306
  (1 shorter events, 0.0 us)
Async XLA Ops:
  0.6 29.2 %copy-start = (bf16[8192]{0:T(1024)(128)(2,1)S(1)}, bf16[8192]{0:T(1024)(128)(2,1)}, u32[]{:S(2)}) copy-start(bf16[8192]{0:T(1024)(128)(2,1)} %param.11) | copy-start | bytes 49156

commit v3 on v2

--- a/solution.py
+++ b/solution.py
@@ -11,6 +11,8 @@
 CORES = 2
 COLUMNS = 512
 LANES = 128
+LAG = 4
+EARLY = 8
 
 
 def block_kernel(
@@ -31,6 +33,8 @@
     keep,
     mate_send,
     mate_recv,
+    early_send,
+    early_recv,
     cross_send,
     cross_recv,
     load_sem,
@@ -40,6 +44,8 @@
     att_recv_sem,
     mate_send_sem,
     mate_recv_sem,
+    early_send_sem,
+    early_recv_sem,
     cross_send_sem,
     cross_recv_sem,
 ):
@@ -55,6 +61,12 @@
     rows = seqs * draft
     chunks, depth, columns = w_buf.shape
     model = chunks * columns
+    half = cross_send.shape[3]
+    halves = rows // half
+    half_seqs = half // draft
+    early = early_send.shape[0] if halves > 1 and chips > 1 else 0
+    ring = keep.shape[0]
+    lag = ring - 1
 
     me = lax.axis_index("tp")
     chip, core = me // CORES, me % CORES
@@ -122,97 +134,164 @@
             device_id_type=pl.DeviceIdType.MESH,
         )
 
-    for step, (dx, dk) in enumerate(order):
+    cross_steps = list(range(len(order) - CORES))
+    near_steps = list(range(len(order) - CORES, len(order)))
+    todo = [(step, s) for s in range(seqs) for step in cross_steps]
+    todo += [(step, s) for step in near_steps for s in range(seqs)]
+    loaded = set()
+    for step, s in todo:
+        dx, dk = order[step]
         slot = slot_of(dx, dk)
         dest = device(dx, dk)
-        kv_copies[step].wait()
+        if step not in loaded:
+            kv_copies[step].wait()
+            loaded.add(step)
         target = att if slot == 0 else att_send
-        for s in range(seqs):
-            for u in range(units):
-                kv_at = u if own_heads >= group else 0
-                start = pl.multiple_of((dest * own_heads + u * unit_heads) * head_dim, LANES)
-                wide = q_buf[s, :, pl.ds(start, unit_heads * head_dim)]
-                q_rows = jnp.concatenate(
-                    [wide[:, h * head_dim : (h + 1) * head_dim] for h in range(unit_heads)], axis=0
-                )
-                keys = kv_buf[step, s, kv_at, :, :head_dim]
-                values = kv_buf[step, s, kv_at, :, head_dim:]
-                scores = lax.dot_general(
-                    q_rows, keys, (((1,), (1,)), ((), ())), preferred_element_type=jnp.float32
-                )
-                scores = scores.reshape(unit_heads, draft, slots_kv) + biases[s][None]
-                peak = jnp.max(scores, axis=-1, keepdims=True)
-                raised = jnp.exp2((scores - peak) * factor)
-                totals = jnp.sum(raised, axis=-1, keepdims=True)
-                out = jnp.dot(
-                    raised.astype(jnp.bfloat16).reshape(unit_heads * draft, slots_kv),
-                    values,
-                    preferred_element_type=jnp.float32,
-                )
-                out = (out * (1.0 / totals).reshape(unit_heads * draft, 1)).astype(jnp.bfloat16)
-                for h in range(unit_heads):
-                    at = (u * unit_heads + h) * head_dim
-                    target[slot, s * draft : (s + 1) * draft, at : at + head_dim] = out[
-                        h * draft : (h + 1) * draft
-                    ]
-            if slot:
-                att_copy(dx, dk, s, slot, slot_of((chips - dx) % chips, dk)).start()
-
-    for dx, dk in order[:-1]:
+        for u in range(units):
+            kv_at = u if own_heads >= group else 0
+            start = pl.multiple_of((dest * own_heads + u * unit_heads) * head_dim, LANES)
+            wide = q_buf[s, :, pl.ds(start, unit_heads * head_dim)]
+            q_rows = jnp.concatenate(
+                [wide[:, h * head_dim : (h + 1) * head_dim] for h in range(unit_heads)], axis=0
+            )
+            keys = kv_buf[step, s, kv_at, :, :head_dim]
+            values = kv_buf[step, s, kv_at, :, head_dim:]
+            scores = lax.dot_general(
+                q_rows, keys, (((1,), (1,)), ((), ())), preferred_element_type=jnp.float32
+            )
+            scores = scores.reshape(unit_heads, draft, slots_kv) + biases[s][None]
+            peak = jnp.max(scores, axis=-1, keepdims=True)
+            raised = jnp.exp2((scores - peak) * factor)
+            totals = jnp.sum(raised, axis=-1, keepdims=True)
+            out = jnp.dot(
+                raised.astype(jnp.bfloat16).reshape(unit_heads * draft, slots_kv),
+                values,
+                preferred_element_type=jnp.float32,
+            )
+            out = (out * (1.0 / totals).reshape(unit_heads * draft, 1)).astype(jnp.bfloat16)
+            for h in range(unit_heads):
+                at = (u * unit_heads + h) * head_dim
+                target[slot, s * draft : (s + 1) * draft, at : at + head_dim] = out[
+                    h * draft : (h + 1) * draft
+                ]
+        if slot:
+            att_copy(dx, dk, s, slot, slot_of((chips - dx) % chips, dk)).start()
+
+    def arrived(step, s):
+        dx, dk = order[step]
         slot = slot_of(dx, dk)
-        for s in range(seqs):
-            att_copy(dx, dk, s, slot, slot).wait_recv()
-
-    def mate_copy(c):
+        att_copy(dx, dk, s, slot, slot).wait_recv()
+
+    def to_mate(source, target, send_sem, recv_sem, c):
         return pltpu.make_async_remote_copy(
-            src_ref=mate_send.at[c],
-            dst_ref=mate_recv.at[c],
-            send_sem=mate_send_sem.at[c],
-            recv_sem=mate_recv_sem.at[c],
+            src_ref=source.at[c],
+            dst_ref=target.at[c],
+            send_sem=send_sem.at[c],
+            recv_sem=recv_sem.at[c],
             device_id={"tp": device(0, 1)},
             device_id_type=pl.DeviceIdType.MESH,
         )
 
-    def cross_copy(dx, source, target, c):
+    mate_copy = functools.partial(to_mate, mate_send, mate_recv, mate_send_sem, mate_recv_sem)
+    early_copy = functools.partial(to_mate, early_send, early_recv, early_send_sem, early_recv_sem)
+
+    def cross_copy(dx, source, target, c, h):
         return pltpu.make_async_remote_copy(
-            src_ref=cross_send.at[source, c],
-            dst_ref=cross_recv.at[target, c],
-            send_sem=cross_send_sem.at[source, c],
-            recv_sem=cross_recv_sem.at[target, c],
+            src_ref=cross_send.at[source, c, h],
+            dst_ref=cross_recv.at[target, c, h],
+            send_sem=cross_send_sem.at[source, c, h],
+            recv_sem=cross_recv_sem.at[target, c, h],
             device_id={"tp": device(dx, 0)},
             device_id_type=pl.DeviceIdType.MESH,
         )
 
+    def send_sum(dx, c, h, mine, mates):
+        cross_send[dx - 1, c, h] = (mine + mates.astype(jnp.float32)).astype(jnp.bfloat16)
+        cross_copy(dx, dx - 1, chips - dx - 1, c, h).start()
+
+    if early:
+        for s in range(half_seqs):
+            for step in cross_steps:
+                arrived(step, s)
+
+        def early_multiply(c):
+            w_copy(c).wait()
+            first = att[CORES:, :half].reshape((n - CORES) * half, depth)
+            product = jnp.dot(first, w_buf[c], preferred_element_type=jnp.float32)
+            for dx in range(1, chips):
+                own = (slot_of(dx, 0) - CORES) * half
+                other = (slot_of(dx, 1) - CORES) * half
+                early_send[c, dx - 1] = product[other : other + half].astype(jnp.bfloat16)
+                keep[c % ring, dx, :half] = product[own : own + half]
+            early_copy(c).start()
+
+        def early_pass(c):
+            early_copy(c).wait_recv()
+            for dx in range(1, chips):
+                send_sum(dx, c, 0, keep[c % ring, dx, :half], early_recv[c, dx - 1])
+
+        def early_step(c, carry):
+            @pl.when(c < early)
+            def _():
+                early_multiply(c)
+
+            @pl.when(c >= lag)
+            def _():
+                early_pass(c - lag)
+
+            return carry
+
+        lax.fori_loop(0, early + lag, early_step, 0)
+
+    for s in range(half_seqs if early else 0, seqs):
+        for step in cross_steps:
+            arrived(step, s)
+    for s in range(seqs):
+        arrived(near_steps[0], s)
+
     def multiply(c):
-        w_copy(c).wait()
+        @pl.when(c >= early)
+        def _():
+            w_copy(c).wait()
+
         product = jnp.dot(
             att[...].reshape(n * rows, depth), w_buf[c], preferred_element_type=jnp.float32
         )
         for dx in range(chips):
             own, other = slot_of(dx, 0) * rows, slot_of(dx, 1) * rows
             mate_send[c, dx] = product[other : other + rows].astype(jnp.bfloat16)
-            keep[c % 2, dx] = product[own : own + rows]
+            keep[c % ring, dx] = product[own : own + rows]
         mate_copy(c).start()
 
     def pass_on(c):
         mate_copy(c).wait_recv()
         for dx in range(1, chips):
-            both = keep[c % 2, dx] + mate_recv[c, dx].astype(jnp.float32)
-            cross_send[dx - 1, c] = both.astype(jnp.bfloat16)
-            cross_copy(dx, dx - 1, chips - dx - 1, c).start()
+            for h in range(halves):
+                part = pl.ds(h * half, half)
+
+                def send():
+                    send_sum(dx, c, h, keep[c % ring, dx, part], mate_recv[c, dx, part])
+
+                if h == 0 and early:
+                    pl.when(c >= early)(send)
+                else:
+                    send()
         at = pl.multiple_of(c * columns, LANES)
-        own = keep[c % 2, 0] + mate_recv[c, 0].astype(jnp.float32)
+        own = keep[c % ring, 0] + mate_recv[c, 0].astype(jnp.float32)
         acc[:, :, pl.ds(at, columns)] = own.reshape(seqs, draft, columns)
 
-    multiply(0)
-
     def both_steps(c, carry):
-        multiply(c)
-        pass_on(c - 1)
+        @pl.when(c < chunks)
+        def _():
+            multiply(c)
+
+        @pl.when(c >= lag)
+        def _():
+            pass_on(c - lag)
+
         return carry
 
-    lax.fori_loop(1, chunks, both_steps, 0)
-    pass_on(chunks - 1)
+    lax.fori_loop(0, chunks + lag, both_steps, 0)
 
     res_copy.wait()
 
@@ -220,7 +299,8 @@
         at = pl.multiple_of(c * columns, LANES)
         total = acc[:, :, pl.ds(at, columns)]
         for dx in range(1, chips):
-            cross_copy(dx, dx - 1, dx - 1, c).wait_recv()
+            for h in range(halves):
+                cross_copy(dx, dx - 1, dx - 1, c, h).wait_recv()
             part = cross_recv[dx - 1, c].astype(jnp.float32)
             total = total + part.reshape(seqs, draft, columns)
         total = total + res_buf[:, :, pl.ds(at, columns)].astype(jnp.float32)
@@ -248,10 +328,13 @@
     def settle(c, carry):
         mate_copy(c).wait_send()
         for dx in range(1, chips):
-            cross_copy(dx, dx - 1, dx - 1, c).wait_send()
+            for h in range(halves):
+                cross_copy(dx, dx - 1, dx - 1, c, h).wait_send()
         return carry
 
     lax.fori_loop(0, chunks, settle, 0)
+    for c in range(early):
+        early_copy(c).wait_send()
 
 
 def on_device(n, queries, kv_cache, lengths, residual, out_weight, norm_gain):
@@ -265,6 +348,10 @@
     columns = math.gcd(model, COLUMNS)
     chunks = model // columns
     kv_per_dest = max(1, kv_heads // n)
+    half = rows // 2 if seqs % 2 == 0 else rows
+    halves = rows // half
+    early = min(EARLY, chunks)
+    others = max(1, chips - 1)
     bf16, f32 = jnp.bfloat16, jnp.float32
     dma = pltpu.SemaphoreType.DMA
     summed, scaled = pl.pallas_call(
@@ -283,11 +370,13 @@
             pltpu.VMEM((chunks, depth, columns), bf16),
             pltpu.VMEM((n, rows, depth), bf16),
             pltpu.VMEM((n, rows, depth), bf16),
-            pltpu.VMEM((2, chips, rows, columns), f32),
+            pltpu.VMEM((LAG + 1, chips, rows, columns), f32),
             pltpu.VMEM((chunks, chips, rows, columns), bf16),
             pltpu.VMEM((chunks, chips, rows, columns), bf16),
-            pltpu.VMEM((max(1, chips - 1), chunks, rows, columns), bf16),
-            pltpu.VMEM((max(1, chips - 1), chunks, rows, columns), bf16),
+            pltpu.VMEM((early, others, half, columns), bf16),
+            pltpu.VMEM((early, others, half, columns), bf16),
+            pltpu.VMEM((others, chunks, halves, half, columns), bf16),
+            pltpu.VMEM((others, chunks, halves, half, columns), bf16),
             dma((2,)),
             dma((n,)),
             dma((chunks,)),
@@ -295,8 +384,10 @@
             dma((n, seqs)),
             dma((chunks,)),
             dma((chunks,)),
-            dma((max(1, chips - 1), chunks)),
-            dma((max(1, chips - 1), chunks)),
+            dma((early,)),
+            dma((early,)),
+            dma((others, chunks, halves)),
+            dma((others, chunks, halves)),
         ],
         compiler_params=pltpu.CompilerParams(
             collective_id=0, has_side_effects=True, vmem_limit_bytes=56 * 1024 * 1024

time: 30.8 us -> 32.2 us (1.045)
  Pallas kernels: 28.3 us -> 29.7 us
    pallas_call x1, Pallas kernels: 28.3 us -> 29.7 us  [on_device(): pl.pallas_call(functools.partial(block_kernel, n), out_shape=(pltpu.VMEM(...]
where the time goes in v3:
time: 32.2 us; the launch traced here: 32 us
  Pallas kernels  29.7 us (92%)
  other arithmetic  1.71 us (5%)
  between operations  0.65 us (2%)
    pallas_call x1, Pallas kernels, on_device(): pl.pallas_call(functools.partial(block_kernel, n), out_shape=(pltpu.VMEM(...  29.7 us
    convert_element_type x2, other arithmetic, on_device(): return (summed.astype(bf16), normed.astype(bf16))  1.71 us

profile of v3, /device:TPU:0, one launch (start us, length us, event | category | flops | bytes accessed | tf_op | source)
XLA Modules:
  0.0 32.0 jit_solution(6443952665680482519)
XLA Ops:
  0.6 0.0 copy-start
  0.6 29.7 %shard_map.77 = (f32[2,16,8192]{2,1,0:T(8,128)S(1)}, f32[2,16,8192]{2,1,0:T(8,128)S(1)}) custom-call(s32[2]{0:T(128)} %lengths_ref.1, bf16[2,16,8192]{2,1,0:T(8,128)(2,1)} %queries_ref.1, bf16[2,8,384,256]{3,2,1,0:T(8,128)(2,1)} %kv_ref.1, bf16[2,16,8192]{2,1,0:T(8,128)(2,1)} %residual_ref.1, bf16[2048,8192]{1,0:T(8,128)(2,1)} %weight_ref.1), custom_call_target="tpu_custom_call" | custom-call | tf_op jit(solution)/shard_map/pallas_call | solution.py:357
  30.3 0.8 %convert_element_type.9 = bf16[2,16,8192]{2,1,0:T(8,128)(2,1)} convert(f32[2,16,8192]{2,1,0:T(8,128)S(1)} %get-tuple-element.4) | non-fusion elementwise | flops 262144 | bytes 1572864 | tf_op jit(solution)/shard_map/convert_element_type | solution.py:397
  31.2 0.0 copy-done
  31.2 0.9 %multiply_convert_fusion = bf16[2,16,8192]{2,1,0:T(8,128)(2,1)} fusion(f32[2,16,8192]{2,1,0:T(8,128)S(1)} %get-tuple-element.5, f32[8192]{0:T(1024)S(1)} %convert_element_type.10), kind=kLoop, calls=%fused_computation | loop fusion | flops 524288 | bytes 1605632 | tf_op jit(solution)/shard_map/convert_element_type | solution.py:397
  (1 shorter events, 0.0 us)
Async XLA Ops:
  0.6 30.5 %copy-start = (bf16[8192]{0:T(1024)(128)(2,1)S(1)}, bf16[8192]{0:T(1024)(128)(2,1)}, u32[]{:S(2)}) copy-start(bf16[8192]{0:T(1024)(128)(2,1)} %param.11) | copy-start | bytes 49156
